TPU v7x, 512 devices: a whole 4x4x16 slice. The times are simulated.
512 devices in a mesh: frow: 32 (over z_lo, y, core), fcol: 16 (over z_hi, x).
Axes of the slice: x: 4, y: 4, z: 16 (z_hi: 4, z_lo: 4; z = z_hi * 4 + z_lo), core: 2. Of those that a mesh axis runs over, the one named last changes fastest.
Arguments:
- model_image: bfloat16 [16384, 16384], P('frow', 'fcol'), may hold values from -6 to 6
- weight_grids: bfloat16 [8, 256, 256], replicated, may hold values from 0.19921875 to 2
- strip_offsets: int32 [2], replicated, may hold values from 0 to 63
- subgrid_offsets: int32 [2, 32], replicated, may hold values from 0 to 63
- grid_index: int32 [2, 32], replicated, may hold values from 0 to 7
Outputs:
- residual_update: float32 [16384, 16384], P('frow', 'fcol')
Inputs may be any that keep to these rules, and one draw needn't show every extreme that they name: `strip_offsets`: two strips may coincide. `subgrid_offsets`: two subgrids of one strip may coincide.
All inputs are finite; a program needn't handle non-finite values.
Results may differ from a plain program's by a relative error of at most 0.03.
Values may be sent and summed in bfloat16 or wider, within the bound.
No kernel may reach another device: no remote copies, remote signals or barrier semaphores. Data moves between devices by JAX's collectives and lax.ppermute only.
A program may use at most 64 MiB of HBM per device.

v0:
```python
import math
import jax
import jax.numpy as jnp
import numpy as np
from jax import lax
from jax.sharding import Mesh
from jax.sharding import PartitionSpec as P

F32 = jnp.float32
BF16 = jnp.bfloat16
STRIP = 256
SUB = 256
AXES = ("zl", "y", "core", "zh", "x")
NEAR = ("zl", "y", "x")


def turn(numerator, denominator):
    angle = (numerator % denominator).astype(F32) * (2.0 * math.pi / denominator)
    return (jnp.cos(angle), jnp.sin(angle))


def tables(quads, blocks, sub_cols, uv_cols):
    r = np.arange(STRIP).reshape(quads, 1, -1, 1, 1)
    p = np.arange(2).reshape(1, 2, 1, 1, 1)
    q = np.arange(2).reshape(1, 1, 1, 2, 1)
    b = np.arange(STRIP).reshape(1, 1, 1, 1, -1)
    phase = 2.0 * np.pi * (r * b % STRIP) / STRIP + (p - q) * (np.pi / 2)
    phase = phase.reshape(2 * STRIP, 2 * STRIP)
    rows = (np.cos(phase), -np.sin(phase))
    d = np.arange(SUB)
    phase = 2.0 * np.pi * (np.outer(d, d) % SUB) / SUB
    cos, sin = (np.cos(phase), np.sin(phase))
    cols = np.block([[cos, -sin], [sin, cos]])
    u = np.arange(uv_cols).reshape(1, -1, 1, 1, 1)
    p = np.arange(2).reshape(2, 1, 1, 1, 1)
    c = blocks.reshape(1, 1, -1, 1, 1)
    q = np.arange(2).reshape(1, 1, 1, 2, 1)
    phase = 2.0 * np.pi * (u * c % uv_cols) / uv_cols + (p - q) * (np.pi / 2)
    phase = np.broadcast_to(np.cos(phase), (2, uv_cols, blocks.size, 2, sub_cols))
    return (rows, cols, phase.reshape(2, uv_cols, -1))


def body(model_image, weight_grids, strip_offsets, subgrid_offsets, grid_index):
    rows_local, facet_width = model_image.shape
    ny, nx, nzl, nzh = (lax.axis_size(a) for a in ("y", "x", "zl", "zh"))
    ncore = lax.axis_size("core")
    zl, y, core, zh, x = (lax.axis_index(a) for a in AXES)
    width = facet_width // ny
    modulus = facet_width * nx * nzh
    uv_cols = modulus // SUB
    periods = rows_local // STRIP
    quads = nzl * ny * nx
    rows_each = STRIP // quads
    count = subgrid_offsets.shape[1]
    strips = strip_offsets.shape[0]
    order = np.arange(uv_cols).reshape(nzh, nx, ny).transpose(0, 2, 1).reshape(-1)
    (rows_cos, rows_sin), cols_table, block_table = tables(quads, order, rows_each, uv_cols)
    own, other = (core, 1 - core)
    offset_own = lax.dynamic_index_in_dim(strip_offsets, own, 0, keepdims=False)
    offset_other = lax.dynamic_index_in_dim(strip_offsets, other, 0, keepdims=False)
    span = (zl * ny + jnp.arange(ny, dtype=jnp.int32)) * ncore + core
    span = span[:, None] * periods + jnp.arange(periods, dtype=jnp.int32)
    own_cos, own_sin = turn(offset_own * span, uv_cols)
    other_cos, other_sin = turn(offset_other * span, uv_cols)
    cos_b, sin_b = turn(offset_own * jnp.arange(STRIP, dtype=jnp.int32), modulus)
    cos_b = jnp.concatenate([cos_b, cos_b])[None]
    sin_b = jnp.concatenate([sin_b, sin_b])[None]
    row_phases = (
        jnp.asarray(rows_cos, BF16).astype(F32) * cos_b
        + jnp.asarray(rows_sin, BF16).astype(F32) * sin_b
    ).astype(BF16)
    gathered = lax.all_to_all(model_image, "y", 1, 0, tiled=True)
    pixels = gathered.reshape(ny, periods, STRIP, width).astype(F32)

    def fold(cos, sin):
        real = jnp.sum(pixels * cos[:, :, None, None], axis=(0, 1))
        imag = -jnp.sum(pixels * sin[:, :, None, None], axis=(0, 1))
        return jnp.concatenate([real, imag], axis=0)

    swap = [(0, 1), (1, 0)]
    received = lax.ppermute(fold(other_cos, other_sin).astype(BF16), "core", swap)
    folded = (fold(own_cos, own_sin) + received.astype(F32)).astype(BF16)
    partial = jnp.dot(row_phases, folded, preferred_element_type=F32).astype(BF16)
    parts = lax.all_to_all(partial.reshape(quads, 2 * rows_each, width), NEAR, 0, 0, tiled=True)
    parts = parts.reshape(nzl, ny * nx, 2 * rows_each, width).astype(F32)
    strip = jnp.sum(parts, axis=0).astype(BF16).reshape(ny * nx * 2 * rows_each, width)
    whole = lax.all_gather(strip, "zh", axis=0, tiled=True)
    quad = (zl * ny + y) * nx + x
    shifts = lax.dynamic_index_in_dim(subgrid_offsets, own, 0, keepdims=False)
    chosen = lax.dynamic_index_in_dim(grid_index, own, 0, keepdims=False)
    lines = rows_each * count
    line_shift = jnp.tile(shifts, rows_each)
    line_row = jnp.repeat(jnp.arange(rows_each, dtype=jnp.int32), count)
    pick = (line_shift[:, None] == jnp.arange(uv_cols, dtype=jnp.int32)[None]).astype(BF16)
    table_row = jnp.arange(2 * uv_cols * rows_each, dtype=jnp.int32) % rows_each
    same = line_row[:, None] == table_row[None]
    spread = [
        jnp.where(
            same,
            jnp.dot(pick, jnp.asarray(block_table[part], BF16), preferred_element_type=F32),
            0.0,
        )
        for part in range(2)
    ]
    spread = jnp.concatenate(spread, axis=0).astype(BF16)
    cos_d, sin_d = turn(shifts[:, None] * jnp.arange(SUB, dtype=jnp.int32)[None], modulus)
    cos_d = jnp.tile(cos_d, (rows_each, 1))
    sin_d = jnp.tile(sin_d, (rows_each, 1))
    fourier = jnp.asarray(cols_table, BF16)
    mixed = jnp.dot(spread, whole, preferred_element_type=F32)
    real, imag = (mixed[:lines], mixed[lines:])
    turned = jnp.concatenate(
        [real * cos_d + imag * sin_d, imag * cos_d - real * sin_d], axis=1
    ).astype(BF16)
    spectra = jnp.dot(turned, fourier, preferred_element_type=F32)
    grid_rows = lax.dynamic_slice_in_dim(weight_grids, quad * rows_each, rows_each, 1)
    grids = grid_rows.shape[0]
    line_grid = jnp.tile(chosen, rows_each)[:, None] * rows_each + line_row[:, None]
    select = (line_grid == jnp.arange(grids * rows_each, dtype=jnp.int32)[None]).astype(BF16)
    weights = jnp.dot(select, grid_rows.reshape(grids * rows_each, SUB), preferred_element_type=F32)
    weighted = (spectra * jnp.concatenate([weights, weights], axis=1)).astype(BF16)
    returned = lax.dot_general(
        weighted, fourier, (((1,), (1,)), ((), ())), preferred_element_type=F32
    )
    real, imag = (returned[:, :SUB], returned[:, SUB:])
    turned = jnp.concatenate(
        [real * cos_d - imag * sin_d, imag * cos_d + real * sin_d], axis=0
    ).astype(BF16)
    held = strip.shape[0]
    mine = lax.dynamic_slice_in_dim(spread, zh * held, held, 1)
    back = lax.dot_general(mine, turned, (((0,), (0,)), ((), ())), preferred_element_type=F32)
    back = back.astype(BF16).reshape(ny * nx, 2 * rows_each, width)
    back = jnp.tile(back, (nzl, 1, 1))
    image = lax.all_to_all(back, NEAR, 0, 0, tiled=True).reshape(2 * STRIP, width)
    scale = 1.0 / (modulus * math.sqrt(count * SUB) * math.sqrt(strips * STRIP))
    expanded = lax.dot_general(
        row_phases, image, (((0,), (0,)), ((), ())), preferred_element_type=F32
    )
    expanded = (expanded * scale).astype(BF16)
    received = lax.ppermute(expanded, "core", swap)

    def unfold(value, cos, sin):
        value = value.astype(F32)[None, None]
        real, imag = (value[:, :, :STRIP], value[:, :, STRIP:])
        return real * cos[:, :, None, None] - imag * sin[:, :, None, None]

    update = unfold(expanded, own_cos, own_sin) + unfold(received, other_cos, other_sin)
    update = update.astype(BF16).reshape(ny * rows_local, width)
    return lax.all_to_all(update, "y", 0, 1, tiled=True).astype(F32)


def solution(mesh):
    shape = {"zl": 4, "y": 4, "core": 2, "zh": 4, "x": 4}
    finer = Mesh(mesh.devices.reshape(tuple(shape.values())), tuple(shape))
    rows, cols = (("zl", "y", "core"), ("zh", "x"))
    return jax.shard_map(
        body,
        mesh=finer,
        in_specs=(P(rows, cols), P(), P(), P(), P()),
        out_specs=P(rows, cols),
        check_vma=False,
    )
```

profile of v0, /device:TPU:1, one launch (start us, length us, event | category | flops | bytes accessed | tf_op | source)
XLA Modules:
  0.0 139.9 jit_solution(11549442983529142427)
XLA Ops:
  0.0 1.6 %copy.15 = bf16[512,1024]{0,1:T(8,128)(2,1)S(1)} copy(bf16[512,1024]{1,0:T(8,128)(2,1)} %param.10) | data formatting | bytes 2097152 | tf_op args[0]
  1.6 1.3 copy.16
  2.9 5.0 %all-to-all-start = ((bf16[512,4,256]{2,0,1:T(8,128)(2,1)}), bf16[512,4,256]{2,0,1:T(8,128)(2,1)S(1)}, u32[]{:S(2)}, u32[]{:S(2)}) async-start(bf16[512,4,256]{2,0,1:T(8,128)(2,1)} %copy.16), calls=%async_computation | async-start | bytes 2097152 | tf_op jit(solution)/shard_map/all_to_all | solution.py:72
  8.6 1.4 fusion.64
  11.4 6.3 %all-to-all-done = bf16[512,4,256]{2,0,1:T(8,128)(2,1)S(1)} async-done(((bf16[512,4,256]{2,0,1:T(8,128)(2,1)}), bf16[512,4,256]{2,0,1:T(8,128)(2,1)S(1)}, u32[]{:S(2)}, u32[]{:S(2)}) %all-to-all-start) | async-done | bytes 1048608 | tf_op jit(solution)/shard_map/all_to_all | solution.py:72
  17.7 2.5 %fusion.2 = (f32[512,256]{1,0:T(8,128)S(1)}, f32[512,256]{1,0:T(8,128)}, f32[512,256]{1,0:T(8,128)}, f32[512,256]{1,0:T(8,128)}) fusion(bf16[512,4,256]{2,0,1:T(8,128)(2,1)S(1)} %all-to-all-done, f32[4,512]{1,0:T(4,128)S(1)} %bitcast.131, f32[4,512]{1,0:T(4,128)S(1)} %bitcast.129, f32[4,512]{1,0:T(4,128)S(1)} %bitcast.125, f32[4,512]{1,0:T(4,128)S(1)} %bitcast.127), kind=kLoop, calls=%fused_computation.6 | loop fusion | flops 4194304 | bytes 3178496 | tf_op jit(solution)/shard_map/reduce_sum | solution.py:76
  20.3 1.2 reduce_sum.87
  22.2 8.4 %collective-permute-start = (bf16[512,256]{1,0:T(8,128)(2,1)}, bf16[512,256]{1,0:T(8,128)(2,1)}, u32[]{:S(2)}, u32[]{:S(2)}) collective-permute-start(bf16[512,256]{1,0:T(8,128)(2,1)} %pad_maximum_fusion.2), channel_id=1, source_target_pairs={{0,16},{16,0},{1,17},{17,1},{2,18},{18,2},{3,19},{19,3},{4,20},{20... | collective-permute-start | bytes 786440 | tf_op jit(solution)/shard_map/ppermute | solution.py:81
  32.1 1.8 %reduce_sum.81 = f32[256,256]{1,0:T(8,128)} reduce(f32[2,256,256]{2,1,0:T(8,128)} %bitcast.115, f32[]{:T(128)} %constant.111.clone.1), dimensions={0}, to_apply=%region_3.4 | reduce | flops 65536 | bytes 786436 | tf_op jit(solution)/shard_map/reduce_sum | solution.py:77
  36.1 2.0 %fusion.5 = bf16[64,8,256]{2,1,0:T(8,128)(2,1)} fusion(f32[512,512]{1,0:T(8,128)S(1)} %copy-done.1, f32[512,512]{1,0:T(8,128)S(1)} %copy-done.2, f32[512]{0:T(512)S(1)} %pad_maximum_fusion.4, f32[512]{0:T(512)S(1)} %pad_maximum_fusion.3, f32[256,256]{1,0:T(8,128)S(1)} %neg.6, f32[256,256]{1,0:T(8,128)S(1)} %reduce_sum.62, ...), kind=kOutput, calls=%fused_computation.12 | convolution fusion | flops 135921664 | bytes 3149824 | tf_op jit(solution)/shard_map/dot_general | solution.py:83
  38.1 9.5 %all-to-all-start.1 = ((bf16[64,8,256]{2,1,0:T(8,128)(2,1)}), bf16[64,8,256]{2,1,0:T(8,128)(2,1)S(1)}, u32[]{:S(2)}, u32[]{:S(2)}) async-start(bf16[64,8,256]{2,1,0:T(8,128)(2,1)} %fusion.5), calls=%async_computation.1 | async-start | bytes 524288 | tf_op jit(solution)/shard_map/all_to_all | solution.py:84
  50.9 1.7 %fusion.8 = bf16[128,512]{1,0:T(8,128)(2,1)} fusion(bf16[64,512]{1,0:T(8,128)(2,1)} %constant.128.clone, s32[512]{0:T(512)S(1)} %add_select_fusion.3, s32[128]{0:T(128)} %copy-done.10, s32[128]{0:T(128)} %eq.66), kind=kOutput, calls=%fused_computation.18 | convolution fusion | flops 8593408 | bytes 199680 | tf_op jit(solution)/shard_map/dot_general | solution.py:100
  52.6 1.7 %fusion.7 = bf16[128,512]{1,0:T(8,128)(2,1)} fusion(bf16[64,512]{1,0:T(8,128)(2,1)} %constant.127.clone, s32[512]{0:T(512)S(1)} %add_select_fusion.3, s32[128]{0:T(128)} %copy-done.10, s32[128]{0:T(128)} %eq.66), kind=kOutput, calls=%fused_computation.17 | convolution fusion | flops 8593408 | bytes 199680 | tf_op jit(solution)/shard_map/dot_general | solution.py:100
  54.3 5.2 %all-to-all-done.1 = bf16[64,8,256]{2,1,0:T(8,128)(2,1)S(1)} async-done(((bf16[64,8,256]{2,1,0:T(8,128)(2,1)}), bf16[64,8,256]{2,1,0:T(8,128)(2,1)S(1)}, u32[]{:S(2)}, u32[]{:S(2)}) %all-to-all-start.1) | async-done | bytes 262176 | tf_op jit(solution)/shard_map/all_to_all | solution.py:84
  60.2 22.4 %all_gather.3 = bf16[512,256]{1,0:T(8,128)(2,1)S(1)} all-gather(bf16[128,256]{1,0:T(8,128)(2,1)} %bitcast.124), channel_id=1, replica_groups=mesh['zl'=4,'y'=4,'core'=2,'zh'=4,'x'=4] {'zh'}, dimensions={0}, use_global_device_ids=true | all-gather | bytes 327680 | tf_op jit(solution)/shard_map/all_gather | solution.py:87
  83.8 1.4 %fusion.26 = (bf16[128,256]{1,0:T(8,128)(2,1)}, bf16[128,256]{1,0:T(8,128)(2,1)S(1)}) fusion(f32[256,256]{1,0:T(8,128)S(1)} %fusion.17, f32[32,256]{1,0:T(8,128)} %get-tuple-element.18, f32[32,256]{1,0:T(8,128)} %get-tuple-element.17), kind=kLoop, calls=%fused_computation.57 | loop fusion | flops 262144 | bytes 458752 | tf_op jit(solution)/shard_map/convert.9
  85.2 1.8 %fusion.75 = f32[128,512]{1,0:T(8,128)} fusion(bf16[128,256]{1,0:T(8,128)(2,1)S(1)} %get-tuple-element.16, bf16[256,512]{1,0:T(8,128)(2,1)} %constant.132), kind=kOutput, calls=%fused_computation.132 | convolution fusion | flops 33554432 | bytes 589824 | tf_op jit(solution)/shard_map/dot_general | solution.py:115
  87.0 1.6 %fusion.10 = f32[128,512]{1,0:T(8,128)S(1)} fusion(bf16[512,512]{1,0:T(8,128)(2,1)} %constant.129.clone, f32[128,512]{1,0:T(8,128)} %fusion.75, bf16[128,256]{1,0:T(8,128)(2,1)} %get-tuple-element.15, bf16[256,512]{1,0:T(8,128)(2,1)} %constant.133, f32[128,256]{1,0:T(8,128)S(1)} %fusion.36), kind=kOutput, calls=%fused_computation.20 | convolution fusion | flops 100925440 | bytes 1507328 | tf_op jit(solution)/shard_map/dot_general | solution.py:122
  90.5 17.1 %all_to_all.33 = bf16[64,8,256]{2,1,0:T(8,128)(2,1)S(1)} all-to-all(bf16[64,8,256]{2,1,0:T(8,128)(2,1)S(1)} %bitcast.123), channel_id=1, replica_groups=mesh['zl'=4,'y'=4,'core'=2,'zh'=4,'x'=4] {'zl','y','x'}, dimensions={0} | all-to-all | bytes 524288 | tf_op jit(solution)/shard_map/all_to_all | solution.py:134
  108.7 6.2 %collective-permute-start.1 = (bf16[512,256]{1,0:T(8,128)(2,1)S(1)}, bf16[512,256]{1,0:T(8,128)(2,1)S(1)}, u32[]{:S(2)}, u32[]{:S(2)}) collective-permute-start(bf16[512,256]{1,0:T(8,128)(2,1)S(1)} %get-tuple-element.26), channel_id=1, source_target_pairs={{0,16},{16,0},{1,17},{17,1},{2,18},{18,2},{3,19},{19,3},{4,20},{20... | collective-permute-start | bytes 786440 | tf_op jit(solution)/shard_map/ppermute | solution.py:140
  118.0 17.2 %all_to_all.34 = bf16[4,512,256]{2,1,0:T(8,128)(2,1)S(1)} all-to-all(bf16[4,512,256]{2,1,0:T(8,128)(2,1)S(1)} %add_convert_fusion), channel_id=1, replica_groups=mesh['zl'=4,'y'=4,'core'=2,'zh'=4,'x'=4] {'y'}, dimensions={0} | all-to-all | bytes 2097152 | tf_op jit(solution)/shard_map/all_to_all | solution.py:149
  135.3 1.3 copy.17
  136.6 1.5 %convert_element_type.115 = f32[4,512,256]{1,2,0:T(8,128)S(1)} convert(bf16[4,512,256]{1,2,0:T(8,128)(2,1)} %copy.17) | non-fusion elementwise | flops 524288 | bytes 3145728 | tf_op jit(solution)/shard_map/convert_element_type | solution.py:149
  138.1 1.8 %copy.18 = f32[512,1024]{1,0:T(8,128)} copy(f32[512,1024]{0,1:T(8,128)S(1)} %bitcast.112) | data formatting | bytes 4194304 | tf_op jit(solution)/shard_map/convert_element_type | solution.py:149
  (71 shorter events, 17.5 us)
Async XLA Ops:
  0.0 32.1 %copy-start = (bf16[8,256,256]{2,1,0:T(8,128)(2,1)S(1)}, bf16[8,256,256]{2,1,0:T(8,128)(2,1)}, u32[]{:S(2)}) copy-start(bf16[8,256,256]{2,1,0:T(8,128)(2,1)} %param.11) | copy-start | bytes 3145732
  1.6 6.3 %copy-start.9 = (s32[2]{0:T(128)S(1)}, s32[2]{0:T(128)}, u32[]{:S(2)}) copy-start(s32[2]{0:T(128)} %param.12) | copy-start | bytes 28
  2.9 14.8 %all-to-all-start = ((bf16[512,4,256]{2,0,1:T(8,128)(2,1)}), bf16[512,4,256]{2,0,1:T(8,128)(2,1)S(1)}, u32[]{:S(2)}, u32[]{:S(2)}) async-start(bf16[512,4,256]{2,0,1:T(8,128)(2,1)} %copy.16), calls=%async_computation | async-start | bytes 2097152 | tf_op jit(solution)/shard_map/all_to_all | solution.py:72
  10.1 10.0 %copy-start.3 = (f32[1,4,2,256]{3,1,2,0:T(4,128)}, f32[1,4,2,256]{3,1,2,0:T(4,128)S(1)}, u32[]{:S(2)}) copy-start(f32[1,4,2,256]{3,1,2,0:T(4,128)S(1)} %copy.22) | copy-start | bytes 24580
  10.2 10.0 %copy-start.5 = (f32[1,4,2,256]{3,1,2,0:T(4,128)}, f32[1,4,2,256]{3,1,2,0:T(4,128)S(1)}, u32[]{:S(2)}) copy-start(f32[1,4,2,256]{3,1,2,0:T(4,128)S(1)} %copy.21) | copy-start | bytes 24580
  20.2 15.8 %copy-start.1 = (f32[512,512]{1,0:T(8,128)S(1)}, f32[512,512]{1,0:T(8,128)}, u32[]{:S(2)}) copy-start(f32[512,512]{1,0:T(8,128)} %constant.131) | copy-start | bytes 3145732
  20.2 15.8 %copy-start.2 = (f32[512,512]{1,0:T(8,128)S(1)}, f32[512,512]{1,0:T(8,128)}, u32[]{:S(2)}) copy-start(f32[512,512]{1,0:T(8,128)} %constant.130) | copy-start | bytes 3145732
  22.2 13.8 %collective-permute-start = (bf16[512,256]{1,0:T(8,128)(2,1)}, bf16[512,256]{1,0:T(8,128)(2,1)}, u32[]{:S(2)}, u32[]{:S(2)}) collective-permute-start(bf16[512,256]{1,0:T(8,128)(2,1)} %pad_maximum_fusion.2), channel_id=1, source_target_pairs={{0,16},{16,0},{1,17},{17,1},{2,18},{18,2},{3,19},{19,3},{4,20},{20... | collective-permute-start | bytes 786440 | tf_op jit(solution)/shard_map/ppermute | solution.py:81
  31.4 6.7 %copy-start.7 = (f32[512]{0:T(512)}, f32[512]{0:T(512)S(1)}, u32[]{:S(2)}) copy-start(f32[512]{0:T(512)S(1)} %pad_maximum_fusion.4) | copy-start | bytes 6148
  32.1 6.0 %copy-start.8 = (f32[512]{0:T(512)}, f32[512]{0:T(512)S(1)}, u32[]{:S(2)}) copy-start(f32[512]{0:T(512)S(1)} %pad_maximum_fusion.3) | copy-start | bytes 6148
  35.1 12.6 %copy-start.11 = (s32[2,32]{1,0:T(2,128)S(1)}, s32[2,32]{1,0:T(2,128)}, u32[]{:S(2)}) copy-start(s32[2,32]{1,0:T(2,128)} %param.13) | copy-start | bytes 772
  35.1 12.6 %copy-start.12 = (s32[2,32]{1,0:T(2,128)S(1)}, s32[2,32]{1,0:T(2,128)}, u32[]{:S(2)}) copy-start(s32[2,32]{1,0:T(2,128)} %param.14) | copy-start | bytes 772
  38.1 21.4 %all-to-all-start.1 = ((bf16[64,8,256]{2,1,0:T(8,128)(2,1)}), bf16[64,8,256]{2,1,0:T(8,128)(2,1)S(1)}, u32[]{:S(2)}, u32[]{:S(2)}) async-start(bf16[64,8,256]{2,1,0:T(8,128)(2,1)} %fusion.5), calls=%async_computation.1 | async-start | bytes 524288 | tf_op jit(solution)/shard_map/all_to_all | solution.py:84
  48.5 0.6 copy-start.10
  108.7 7.4 %collective-permute-start.1 = (bf16[512,256]{1,0:T(8,128)(2,1)S(1)}, bf16[512,256]{1,0:T(8,128)(2,1)S(1)}, u32[]{:S(2)}, u32[]{:S(2)}) collective-permute-start(bf16[512,256]{1,0:T(8,128)(2,1)S(1)} %get-tuple-element.26), channel_id=1, source_target_pairs={{0,16},{16,0},{1,17},{17,1},{2,18},{18,2},{3,19},{19,3},{4,20},{20... | collective-permute-start | bytes 786440 | tf_op jit(solution)/shard_map/ppermute | solution.py:140
  116.1 0.7 copy-start.4
  116.1 0.7 copy-start.6
where the time goes:
time: 141 us; the launch traced here: 140 us
  blocking collectives  56.7 us (40%)
  starting transfers between devices  29.1 us (21%)
  other arithmetic  19 us (13%)
  matrix products  13.1 us (9%)
  waiting for transfers between devices  12.6 us (9%)
  local copies, waits for them, and re-layouts  9.07 us (6%)
    all_gather x1, blocking collectives, body(): whole = lax.all_gather(strip, 'zh', axis=0, tiled=True)  22.4 us
    all_to_all x1, blocking collectives, body(): return lax.all_to_all(update, 'y', 0, 1, tiled=True).astype(F32)  17.2 us
    all_to_all x1, blocking collectives, body(): lax.all_to_all(back, NEAR, 0, 0, tiled=True).reshape(2 * STRIP, width)  17.1 us
    all_to_all x1, starting transfers between devices, body(): lax.all_to_all(partial.reshape(quads, 2 * rows_each, width), NEAR, 0, 0,...  9.53 us
    ppermute x1, starting transfers between devices, body(): lax.ppermute(fold(other_cos, other_sin).astype(BF16), 'core', swap)  8.36 us
    all_to_all x1, waiting for transfers between devices, body(): gathered = lax.all_to_all(model_image, 'y', 1, 0, tiled=True)  6.31 us
    ppermute x1, starting transfers between devices, body(): received = lax.ppermute(expanded, 'core', swap)  6.21 us
    all_to_all x1, waiting for transfers between devices, body(): lax.all_to_all(partial.reshape(quads, 2 * rows_each, width), NEAR, 0, 0,...  5.2 us
  transfers between devices with their start and end apart: 4, of which 3 were waited for; matrix products, arithmetic and copies ran while one was open for 11% of the time, Pallas kernels for 0%

commit v1 on v0

--- a/solution.py
+++ b/solution.py
@@ -84,7 +84,15 @@
     parts = lax.all_to_all(partial.reshape(quads, 2 * rows_each, width), NEAR, 0, 0, tiled=True)
     parts = parts.reshape(nzl, ny * nx, 2 * rows_each, width).astype(F32)
     strip = jnp.sum(parts, axis=0).astype(BF16).reshape(ny * nx * 2 * rows_each, width)
-    whole = lax.all_gather(strip, "zh", axis=0, tiled=True)
+    whole = jnp.concatenate(
+        jax.lax.all_to_all(
+            jnp.stack(jax.lax.axis_size("zh") * [strip], axis=0),
+            concat_axis=0,
+            axis_name="zh",
+            split_axis=0,
+        ),
+        axis=0,
+    )
     quad = (zl * ny + y) * nx + x
     shifts = lax.dynamic_index_in_dim(subgrid_offsets, own, 0, keepdims=False)
     chosen = lax.dynamic_index_in_dim(grid_index, own, 0, keepdims=False)

time: 141 us -> 149 us (1.057)
  blocking collectives: 56.7 us -> 34.4 us
  waiting for transfers between devices: 12.6 us -> 29.2 us
  starting transfers between devices: 29.1 us -> 42.3 us
    all_gather x1 -> x0, blocking collectives: 22.4 us -> none  [body(): whole = lax.all_gather(strip, 'zh', axis=0, tiled=True)]
    all_to_all x0 -> x1, starting transfers between devices: none -> 12.1 us  [body(): jax.lax.all_to_all(jnp.stack(jax.lax.axis_size('zh') * [strip], axis=0),...]
    all_to_all x0 -> x1, waiting for transfers between devices: none -> 11.6 us  [body(): jax.lax.all_to_all(jnp.stack(jax.lax.axis_size('zh') * [strip], axis=0),...]
    all_to_all x1, waiting for transfers between devices: 5.2 us -> 8.96 us  [body(): lax.all_to_all(partial.reshape(quads, 2 * rows_each, width), NEAR, 0, 0,...]
  transfers between devices with their start and end apart: 4 -> 5, of which waited for: 3 -> 4; matrix products, arithmetic and copies ran while one was open for 11% -> 10% of each run, Pallas kernels for 0% -> 0%
where the time goes in v1:
time: 149 us; the launch traced here: 147 us
  starting transfers between devices  42.3 us (28%)
  blocking collectives  34.4 us (23%)
  waiting for transfers between devices  29.2 us (20%)
  other arithmetic  18.2 us (12%)
  matrix products  13.1 us (9%)
  local copies, waits for them, and re-layouts  9.73 us (7%)
    all_to_all x1, blocking collectives, body(): return lax.all_to_all(update, 'y', 0, 1, tiled=True).astype(F32)  17.2 us
    all_to_all x1, blocking collectives, body(): lax.all_to_all(back, NEAR, 0, 0, tiled=True).reshape(2 * STRIP, width)  17.1 us
    all_to_all x1, starting transfers between devices, body(): jax.lax.all_to_all(jnp.stack(jax.lax.axis_size('zh') * [strip], axis=0),...  12.1 us
    all_to_all x1, waiting for transfers between devices, body(): jax.lax.all_to_all(jnp.stack(jax.lax.axis_size('zh') * [strip], axis=0),...  11.6 us
    all_to_all x1, starting transfers between devices, body(): lax.all_to_all(partial.reshape(quads, 2 * rows_each, width), NEAR, 0, 0,...  9.52 us
    all_to_all x1, waiting for transfers between devices, body(): lax.all_to_all(partial.reshape(quads, 2 * rows_each, width), NEAR, 0, 0,...  8.96 us
    ppermute x1, starting transfers between devices, body(): lax.ppermute(fold(other_cos, other_sin).astype(BF16), 'core', swap)  8.36 us
    all_to_all x1, waiting for transfers between devices, body(): gathered = lax.all_to_all(model_image, 'y', 1, 0, tiled=True)  7.54 us
  transfers between devices with their start and end apart: 5, of which 4 were waited for; matrix products, arithmetic and copies ran while one was open for 10% of the time, Pallas kernels for 0%

profile of v1, /device:TPU:1, one launch (start us, length us, event | category | flops | bytes accessed | tf_op | source)
XLA Modules:
  0.0 147.4 jit_solution(15382442426206237939)
XLA Ops:
  0.0 1.6 %copy.15 = bf16[512,1024]{0,1:T(8,128)(2,1)S(1)} copy(bf16[512,1024]{1,0:T(8,128)(2,1)} %param.10) | data formatting | bytes 2097152 | tf_op args[0]
  1.6 1.3 copy.16
  2.9 5.0 %all-to-all-start = ((bf16[512,4,256]{2,0,1:T(8,128)(2,1)}), bf16[512,4,256]{2,0,1:T(8,128)(2,1)S(1)}, u32[]{:S(2)}, u32[]{:S(2)}) async-start(bf16[512,4,256]{2,0,1:T(8,128)(2,1)} %copy.16), calls=%async_computation | async-start | bytes 2097152 | tf_op jit(solution)/shard_map/all_to_all | solution.py:72
  8.6 1.4 fusion.64
  10.1 7.5 %all-to-all-done = bf16[512,4,256]{2,0,1:T(8,128)(2,1)S(1)} async-done(((bf16[512,4,256]{2,0,1:T(8,128)(2,1)}), bf16[512,4,256]{2,0,1:T(8,128)(2,1)S(1)}, u32[]{:S(2)}, u32[]{:S(2)}) %all-to-all-start) | async-done | bytes 1048608 | tf_op jit(solution)/shard_map/all_to_all | solution.py:72
  17.7 2.7 %fusion.2 = (f32[512,256]{1,0:T(8,128)}, f32[512,256]{1,0:T(8,128)}, f32[512,256]{1,0:T(8,128)}, f32[512,256]{1,0:T(8,128)}) fusion(bf16[512,4,256]{2,0,1:T(8,128)(2,1)S(1)} %all-to-all-done, f32[4,512]{1,0:T(4,128)S(1)} %bitcast.133, f32[4,512]{1,0:T(4,128)S(1)} %bitcast.131, f32[4,512]{1,0:T(4,128)S(1)} %bitcast.127, f32[4,512]{1,0:T(4,128)S(1)} %bitcast.129), kind=kLoop, calls=%fused_computation.6 | loop fusion | flops 4194304 | bytes 3178496 | tf_op jit(solution)/shard_map/reduce_sum | solution.py:76
  23.5 8.4 %collective-permute-start = (bf16[512,256]{1,0:T(8,128)(2,1)}, bf16[512,256]{1,0:T(8,128)(2,1)}, u32[]{:S(2)}, u32[]{:S(2)}) collective-permute-start(bf16[512,256]{1,0:T(8,128)(2,1)} %pad_maximum_fusion.2), channel_id=1, source_target_pairs={{0,16},{16,0},{1,17},{17,1},{2,18},{18,2},{3,19},{19,3},{4,20},{20... | collective-permute-start | bytes 786440 | tf_op jit(solution)/shard_map/ppermute | solution.py:81
  32.6 1.8 %reduce_sum.81 = f32[256,256]{1,0:T(8,128)} reduce(f32[2,256,256]{2,1,0:T(8,128)} %bitcast.116, f32[]{:T(128)} %constant.111.clone.1), dimensions={0}, to_apply=%region_3.4 | reduce | flops 65536 | bytes 786436 | tf_op jit(solution)/shard_map/reduce_sum | solution.py:77
  36.5 2.0 %fusion.5 = bf16[64,8,256]{2,1,0:T(8,128)(2,1)} fusion(f32[512,512]{1,0:T(8,128)S(1)} %copy-done.1, f32[512,512]{1,0:T(8,128)S(1)} %copy-done.2, f32[512]{0:T(512)S(1)} %pad_maximum_fusion.4, f32[512]{0:T(512)S(1)} %pad_maximum_fusion.3, f32[256,256]{1,0:T(8,128)S(1)} %neg.6, f32[256,256]{1,0:T(8,128)S(1)} %reduce_sum.62, ...), kind=kOutput, calls=%fused_computation.12 | convolution fusion | flops 135921664 | bytes 3149824 | tf_op jit(solution)/shard_map/dot_general | solution.py:83
  38.5 9.5 %all-to-all-start.1 = ((bf16[64,8,256]{2,1,0:T(8,128)(2,1)}), bf16[64,8,256]{2,1,0:T(8,128)(2,1)S(1)}, u32[]{:S(2)}, u32[]{:S(2)}) async-start(bf16[64,8,256]{2,1,0:T(8,128)(2,1)} %fusion.5), calls=%async_computation.1 | async-start | bytes 524288 | tf_op jit(solution)/shard_map/all_to_all | solution.py:84
  51.0 9.0 %all-to-all-done.1 = bf16[64,8,256]{2,1,0:T(8,128)(2,1)S(1)} async-done(((bf16[64,8,256]{2,1,0:T(8,128)(2,1)}), bf16[64,8,256]{2,1,0:T(8,128)(2,1)S(1)}, u32[]{:S(2)}, u32[]{:S(2)}) %all-to-all-start.1) | async-done | bytes 262176 | tf_op jit(solution)/shard_map/all_to_all | solution.py:84
  60.7 12.1 %all-to-all-start.2 = ((bf16[4,128,256]{2,1,0:T(8,128)(2,1)}), bf16[4,128,256]{2,1,0:T(8,128)(2,1)S(1)}, u32[]{:S(2)}, u32[]{:S(2)}) async-start(bf16[4,128,256]{2,1,0:T(8,128)(2,1)} %stack.3), calls=%async_computation.2 | async-start | bytes 524288 | tf_op jit(solution)/shard_map/all_to_all | solution.py:88
  73.8 1.7 %fusion.8 = bf16[128,512]{1,0:T(8,128)(2,1)} fusion(bf16[64,512]{1,0:T(8,128)(2,1)} %constant.128.clone, s32[512]{0:T(512)S(1)} %add_select_fusion.3, s32[128]{0:T(128)} %copy-done.10, s32[128]{0:T(128)} %eq.66), kind=kOutput, calls=%fused_computation.18 | convolution fusion | flops 8593408 | bytes 199680 | tf_op jit(solution)/shard_map/dot_general | solution.py:108
  75.5 1.7 %fusion.7 = bf16[128,512]{1,0:T(8,128)(2,1)} fusion(bf16[64,512]{1,0:T(8,128)(2,1)} %constant.127.clone, s32[512]{0:T(512)S(1)} %add_select_fusion.3, s32[128]{0:T(128)} %copy-done.10, s32[128]{0:T(128)} %eq.66), kind=kOutput, calls=%fused_computation.17 | convolution fusion | flops 8593408 | bytes 199680 | tf_op jit(solution)/shard_map/dot_general | solution.py:108
  77.2 11.6 %all-to-all-done.2 = bf16[4,128,256]{2,1,0:T(8,128)(2,1)S(1)} async-done(((bf16[4,128,256]{2,1,0:T(8,128)(2,1)}), bf16[4,128,256]{2,1,0:T(8,128)(2,1)S(1)}, u32[]{:S(2)}, u32[]{:S(2)}) %all-to-all-start.2) | async-done | bytes 262176 | tf_op jit(solution)/shard_map/all_to_all | solution.py:88
  90.1 1.4 fusion.26
  91.5 1.8 %fusion.75 = f32[128,512]{1,0:T(8,128)} fusion(bf16[128,256]{1,0:T(8,128)(2,1)S(1)} %get-tuple-element.16, bf16[256,512]{1,0:T(8,128)(2,1)} %constant.132), kind=kOutput, calls=%fused_computation.132 | convolution fusion | flops 33554432 | bytes 589824 | tf_op jit(solution)/shard_map/dot_general | solution.py:123
  93.3 1.6 %fusion.10 = f32[128,512]{1,0:T(8,128)S(1)} fusion(bf16[512,512]{1,0:T(8,128)(2,1)} %constant.129.clone, f32[128,512]{1,0:T(8,128)} %fusion.75, bf16[128,256]{1,0:T(8,128)(2,1)} %get-tuple-element.15, bf16[256,512]{1,0:T(8,128)(2,1)} %constant.133, f32[128,256]{1,0:T(8,128)S(1)} %fusion.36), kind=kOutput, calls=%fused_computation.20 | convolution fusion | flops 100925440 | bytes 1507328 | tf_op jit(solution)/shard_map/dot_general | solution.py:130
  96.8 17.1 %all_to_all.38 = bf16[64,8,256]{2,1,0:T(8,128)(2,1)S(1)} all-to-all(bf16[64,8,256]{2,1,0:T(8,128)(2,1)S(1)} %bitcast.125), channel_id=1, replica_groups=mesh['zl'=4,'y'=4,'core'=2,'zh'=4,'x'=4] {'zl','y','x'}, dimensions={0} | all-to-all | bytes 524288 | tf_op jit(solution)/shard_map/all_to_all | solution.py:142
  115.1 7.3 %collective-permute-start.1 = (bf16[512,256]{1,0:T(8,128)(2,1)S(1)}, bf16[512,256]{1,0:T(8,128)(2,1)S(1)}, u32[]{:S(2)}, u32[]{:S(2)}) collective-permute-start(bf16[512,256]{1,0:T(8,128)(2,1)S(1)} %get-tuple-element.26), channel_id=1, source_target_pairs={{0,16},{16,0},{1,17},{17,1},{2,18},{18,2},{3,19},{19,3},{4,20},{20... | collective-permute-start | bytes 786440 | tf_op jit(solution)/shard_map/ppermute | solution.py:148
  125.5 17.2 %all_to_all.39 = bf16[4,512,256]{2,1,0:T(8,128)(2,1)S(1)} all-to-all(bf16[4,512,256]{2,1,0:T(8,128)(2,1)S(1)} %add_convert_fusion), channel_id=1, replica_groups=mesh['zl'=4,'y'=4,'core'=2,'zh'=4,'x'=4] {'y'}, dimensions={0} | all-to-all | bytes 2097152 | tf_op jit(solution)/shard_map/all_to_all | solution.py:157
  142.8 1.3 copy.17
  144.1 1.5 %convert_element_type.115 = f32[4,512,256]{1,2,0:T(8,128)S(1)} convert(bf16[4,512,256]{1,2,0:T(8,128)(2,1)} %copy.17) | non-fusion elementwise | flops 524288 | bytes 3145728 | tf_op jit(solution)/shard_map/convert_element_type | solution.py:157
  145.6 1.8 %copy.18 = f32[512,1024]{1,0:T(8,128)} copy(f32[512,1024]{0,1:T(8,128)S(1)} %bitcast.113) | data formatting | bytes 4194304 | tf_op jit(solution)/shard_map/convert_element_type | solution.py:157
  (73 shorter events, 18.5 us)
Async XLA Ops:
  0.0 48.9 %copy-start = (bf16[8,256,256]{2,1,0:T(8,128)(2,1)S(1)}, bf16[8,256,256]{2,1,0:T(8,128)(2,1)}, u32[]{:S(2)}) copy-start(bf16[8,256,256]{2,1,0:T(8,128)(2,1)} %param.11) | copy-start | bytes 3145732
  1.6 6.3 %copy-start.9 = (s32[2]{0:T(128)S(1)}, s32[2]{0:T(128)}, u32[]{:S(2)}) copy-start(s32[2]{0:T(128)} %param.12) | copy-start | bytes 28
  2.9 14.8 %all-to-all-start = ((bf16[512,4,256]{2,0,1:T(8,128)(2,1)}), bf16[512,4,256]{2,0,1:T(8,128)(2,1)S(1)}, u32[]{:S(2)}, u32[]{:S(2)}) async-start(bf16[512,4,256]{2,0,1:T(8,128)(2,1)} %copy.16), calls=%async_computation | async-start | bytes 2097152 | tf_op jit(solution)/shard_map/all_to_all | solution.py:72
  10.1 10.3 %copy-start.3 = (f32[1,4,2,256]{3,1,2,0:T(4,128)}, f32[1,4,2,256]{3,1,2,0:T(4,128)S(1)}, u32[]{:S(2)}) copy-start(f32[1,4,2,256]{3,1,2,0:T(4,128)S(1)} %copy.22) | copy-start | bytes 24580
  10.1 10.2 %copy-start.5 = (f32[1,4,2,256]{3,1,2,0:T(4,128)}, f32[1,4,2,256]{3,1,2,0:T(4,128)S(1)}, u32[]{:S(2)}) copy-start(f32[1,4,2,256]{3,1,2,0:T(4,128)S(1)} %copy.21) | copy-start | bytes 24580
  20.4 16.2 %copy-start.1 = (f32[512,512]{1,0:T(8,128)S(1)}, f32[512,512]{1,0:T(8,128)}, u32[]{:S(2)}) copy-start(f32[512,512]{1,0:T(8,128)} %constant.131) | copy-start | bytes 3145732
  20.4 16.2 %copy-start.2 = (f32[512,512]{1,0:T(8,128)S(1)}, f32[512,512]{1,0:T(8,128)}, u32[]{:S(2)}) copy-start(f32[512,512]{1,0:T(8,128)} %constant.130) | copy-start | bytes 3145732
  23.5 13.1 %collective-permute-start = (bf16[512,256]{1,0:T(8,128)(2,1)}, bf16[512,256]{1,0:T(8,128)(2,1)}, u32[]{:S(2)}, u32[]{:S(2)}) collective-permute-start(bf16[512,256]{1,0:T(8,128)(2,1)} %pad_maximum_fusion.2), channel_id=1, source_target_pairs={{0,16},{16,0},{1,17},{17,1},{2,18},{18,2},{3,19},{19,3},{4,20},{20... | collective-permute-start | bytes 786440 | tf_op jit(solution)/shard_map/ppermute | solution.py:81
  32.6 6.0 %copy-start.7 = (f32[512]{0:T(512)}, f32[512]{0:T(512)S(1)}, u32[]{:S(2)}) copy-start(f32[512]{0:T(512)S(1)} %pad_maximum_fusion.4) | copy-start | bytes 6148
  32.6 5.9 %copy-start.8 = (f32[512]{0:T(512)}, f32[512]{0:T(512)S(1)}, u32[]{:S(2)}) copy-start(f32[512]{0:T(512)S(1)} %pad_maximum_fusion.3) | copy-start | bytes 6148
  35.5 12.6 %copy-start.11 = (s32[2,32]{1,0:T(2,128)S(1)}, s32[2,32]{1,0:T(2,128)}, u32[]{:S(2)}) copy-start(s32[2,32]{1,0:T(2,128)} %param.13) | copy-start | bytes 772
  35.5 12.6 %copy-start.12 = (s32[2,32]{1,0:T(2,128)S(1)}, s32[2,32]{1,0:T(2,128)}, u32[]{:S(2)}) copy-start(s32[2,32]{1,0:T(2,128)} %param.14) | copy-start | bytes 772
  38.5 21.4 %all-to-all-start.1 = ((bf16[64,8,256]{2,1,0:T(8,128)(2,1)}), bf16[64,8,256]{2,1,0:T(8,128)(2,1)S(1)}, u32[]{:S(2)}, u32[]{:S(2)}) async-start(bf16[64,8,256]{2,1,0:T(8,128)(2,1)} %fusion.5), calls=%async_computation.1 | async-start | bytes 524288 | tf_op jit(solution)/shard_map/all_to_all | solution.py:84
  48.9 11.0 %copy-start.10 = (s32[128]{0:T(128)}, s32[128]{0:T(128)S(1)}, u32[]{:S(2)}) copy-start(s32[128]{0:T(128)S(1)} %eq.62) | copy-start | bytes 1540
  60.7 28.2 %all-to-all-start.2 = ((bf16[4,128,256]{2,1,0:T(8,128)(2,1)}), bf16[4,128,256]{2,1,0:T(8,128)(2,1)S(1)}, u32[]{:S(2)}, u32[]{:S(2)}) async-start(bf16[4,128,256]{2,1,0:T(8,128)(2,1)} %stack.3), calls=%async_computation.2 | async-start | bytes 524288 | tf_op jit(solution)/shard_map/all_to_all | solution.py:88
  115.1 8.5 %collective-permute-start.1 = (bf16[512,256]{1,0:T(8,128)(2,1)S(1)}, bf16[512,256]{1,0:T(8,128)(2,1)S(1)}, u32[]{:S(2)}, u32[]{:S(2)}) collective-permute-start(bf16[512,256]{1,0:T(8,128)(2,1)S(1)} %get-tuple-element.26), channel_id=1, source_target_pairs={{0,16},{16,0},{1,17},{17,1},{2,18},{18,2},{3,19},{19,3},{4,20},{20... | collective-permute-start | bytes 786440 | tf_op jit(solution)/shard_map/ppermute | solution.py:148
  123.6 0.7 copy-start.4
  123.6 0.7 copy-start.6
